TPU v7x, 32 devices: a whole 2x2x4 slice. The times are simulated.
32 devices in a mesh: pulse: 4 (over y, x), tile: 8 (over z, core).
Axes of the slice: x: 2, y: 2, z: 4, core: 2. Of those that a mesh axis runs over, the one named last changes fastest.
Arguments:
- pulses: bfloat16 [4096, 2, 4096], P(None, None, ('pulse', 'tile')), may hold values from -6 to 6
- steering: bfloat16 [2, 128, 128], replicated, may hold values from -0.375 to 0.375
- merge_re: bfloat16 [3, 256, 256], replicated, may hold values from -0.25 to 0.25
- merge_im: bfloat16 [3, 256, 256], replicated, may hold values from -0.25 to 0.25
- range_shift: int32 [3, 2, 128], replicated, may hold values from -8 to 8
- image_map: bfloat16 [4, 8, 2, 128, 512], P('pulse', 'tile'), may hold values from -0.0625 to 0.0625
Outputs:
- image: float32 [4096, 1024], P(('pulse', 'tile'))
All inputs are finite; a program needn't handle non-finite values.
Results may differ from a plain program's by a relative error of at most 0.0057.
Values may be sent and summed in bfloat16 or wider, within the bound.
A program may use at most 64 MiB of HBM per device.

v0:
```python
import jax
import jax.numpy as jnp
from jax import lax
from jax.sharding import PartitionSpec as P

SHIFT = 8


def partner_2(value, axis, apart):
    mask = 2**apart
    pairs = [(source, source ^ mask) for source in range(lax.axis_size(axis))]
    return lax.ppermute(value, axis, pairs)


def complex_block(real_part, imag_part):
    upper_half = jnp.concatenate([real_part, imag_part], axis=1)
    lower_half = jnp.concatenate([-imag_part, real_part], axis=1)
    return jnp.concatenate([upper_half, lower_half], axis=0)


def shift_rows(beam_rows, shift_table):
    range_rows = beam_rows.shape[0]
    doubled = jnp.concatenate([shift_table, shift_table])
    padded = jnp.pad(beam_rows, ((SHIFT, SHIFT), (0, 0)))
    result = jnp.zeros_like(beam_rows)
    for offset in range(-SHIFT, SHIFT + 1):
        window = padded[SHIFT + offset : SHIFT + offset + range_rows]
        result = jnp.where(doubled[None, :] == offset, window, result)
    return result


def body(pulses, steering, merge_re, merge_im, range_shift, image_map):
    range_rows = pulses.shape[0]
    beam_count = steering.shape[2]
    group_count = lax.axis_size("pulse")
    tile_count = lax.axis_size("tile")
    pulse_rows = pulses.reshape(range_rows, -1)
    current = jnp.dot(
        pulse_rows, complex_block(steering[0], steering[1]), preferred_element_type=jnp.float32
    ).astype(jnp.bfloat16)
    position = lax.axis_index("tile")
    for merge_level in range(merge_re.shape[0]):
        partner = partner_2(current, "tile", merge_level)
        half_bit = position >> merge_level & 1
        is_upper = half_bit == 1
        lower_src = jnp.where(is_upper, partner, current)
        upper_src = jnp.where(is_upper, current, partner)
        shifted_lower = shift_rows(lower_src, range_shift[merge_level, 0])
        shifted_upper = shift_rows(upper_src, range_shift[merge_level, 1])
        combined = jnp.concatenate(
            [
                shifted_lower[:, :beam_count],
                shifted_upper[:, :beam_count],
                shifted_lower[:, beam_count:],
                shifted_upper[:, beam_count:],
            ],
            axis=1,
        )
        weight_re = lax.dynamic_slice_in_dim(
            merge_re[merge_level], half_bit * beam_count, beam_count, 1
        )
        weight_im = lax.dynamic_slice_in_dim(
            merge_im[merge_level], half_bit * beam_count, beam_count, 1
        )
        current = jnp.dot(
            combined, complex_block(weight_re, weight_im), preferred_element_type=jnp.float32
        ).astype(jnp.bfloat16)
    block_rows = range_rows // (group_count * tile_count)
    arranged = current.reshape(1, group_count, tile_count, block_rows, 2 * beam_count)
    received = lax.all_to_all(arranged, "tile", split_axis=2, concat_axis=0, tiled=True)
    received = received.reshape(tile_count, group_count * block_rows, 2 * beam_count)
    piece = lax.all_gather(image_map, "tile", axis=1, tiled=True)
    blocks = jax.vmap(complex_block)(piece[0][:, 0], piece[0][:, 1])
    partial_rows = jnp.einsum("jrk,jkx->rx", received, blocks, preferred_element_type=jnp.float32)
    result = lax.psum_scatter(partial_rows, "pulse", scatter_dimension=0, tiled=True)
    return result


def solution(mesh):
    placed = (
        P(None, None, ("pulse", "tile")),
        P(),
        P(),
        P(),
        P(),
        P("pulse", "tile", None, None, None),
    )
    return jax.shard_map(
        body, mesh=mesh, in_specs=placed, out_specs=P(("pulse", "tile"), None), check_vma=False
    )
```

profile of v0, /device:TPU:0, one launch (start us, length us, event | category | flops | bytes accessed | tf_op | source)
XLA Modules:
  0.0 387.2 jit_solution(10329893445591188012)
XLA Ops:
  6.5 0.0 all-gather.2.cloned.1.call-start
  6.5 0.8 slice_bitcast_fusion.2
  7.3 0.8 fusion.68
  8.1 0.0 copy-start.3
  8.1 0.0 copy-start.1
  8.1 0.0 copy-start.2
  8.1 2.4 fusion
  10.5 0.6 collective-permute-start
  11.1 0.0 copy-done.3
  11.3 0.0 copy-done.1
  11.3 0.0 copy-done.2
  11.4 3.6 collective-permute-done
  15.0 1.9 broadcast_select_fusion.1
  16.9 16.6 %select_select_fusion.5 = bf16[4096,256]{0,1:T(8,128)(2,1)S(1)} fusion(bf16[4096,256]{0,1:T(8,128)(2,1)S(1)} %get-tuple-element.15, pred[256]{0:T(512)(128)(4,1)S(1)} %get-tuple-element.146, pred[256]{0:T(512)(128)(4,1)S(1)} %get-tuple-element.124, pred[256]{0:T(512)(128)(4,1)S(1)} %get-tuple-element.123, pred[256]{0:T(512)(128)(4,1)S(1)} %get-tuple-element.122, ...), kind=kLoop, calls=%fused_computation.61 | loop fusion | flops 17825792 | bytes 4198656 | tf_op jit(solution)/shard_map/jit(_where)/select_n | solution.py:28
  33.5 0.2 fusion.77
  33.7 16.6 %select_select_fusion.4 = bf16[4096,256]{0,1:T(8,128)(2,1)S(1)} fusion(bf16[4096,256]{0,1:T(8,128)(2,1)S(1)} %get-tuple-element.16, pred[256]{0:T(512)(128)(4,1)S(1)} %get-tuple-element.145, pred[256]{0:T(512)(128)(4,1)S(1)} %get-tuple-element.140, pred[256]{0:T(512)(128)(4,1)S(1)} %get-tuple-element.139, pred[256]{0:T(512)(128)(4,1)S(1)} %get-tuple-element.138, ...), kind=kLoop, calls=%fused_computation.56 | loop fusion | flops 17825792 | bytes 4198656 | tf_op jit(solution)/shard_map/jit(_where)/select_n | solution.py:28
  50.2 0.2 fusion.78
  50.5 1.6 convolution_convert_fusion.2
  52.0 3.0 collective-permute-start.1
  55.2 0.1 fusion.70
  55.3 45.8 %collective-permute-done.1 = bf16[4096,256]{0,1:T(8,128)(2,1)} collective-permute-done((bf16[4096,256]{0,1:T(8,128)(2,1)S(1)}, bf16[4096,256]{0,1:T(8,128)(2,1)}, u32[]{:S(2)}, u32[]{:S(2)}) %collective-permute-start.1) | collective-permute-done | bytes 2097184 | tf_op jit(solution)/shard_map/ppermute | solution.py:12
  101.1 1.9 broadcast_select_fusion.3
  102.9 16.6 %select_select_fusion.3 = bf16[4096,256]{0,1:T(8,128)(2,1)S(1)} fusion(bf16[4096,256]{0,1:T(8,128)(2,1)S(1)} %get-tuple-element.13, pred[256]{0:T(512)(128)(4,1)S(1)} %get-tuple-element.144, pred[256]{0:T(512)(128)(4,1)S(1)} %get-tuple-element.92, pred[256]{0:T(512)(128)(4,1)S(1)} %get-tuple-element.91, pred[256]{0:T(512)(128)(4,1)S(1)} %get-tuple-element.90, ...), kind=kLoop, calls=%fused_computation.51 | loop fusion | flops 17825792 | bytes 4198656 | tf_op jit(solution)/shard_map/jit(_where)/select_n | solution.py:28
  119.5 0.2 fusion.75
  119.7 16.6 %select_select_fusion.2 = bf16[4096,256]{0,1:T(8,128)(2,1)S(1)} fusion(bf16[4096,256]{0,1:T(8,128)(2,1)S(1)} %get-tuple-element.14, pred[256]{0:T(512)(128)(4,1)S(1)} %get-tuple-element.143, pred[256]{0:T(512)(128)(4,1)S(1)} %get-tuple-element.108, pred[256]{0:T(512)(128)(4,1)S(1)} %get-tuple-element.107, pred[256]{0:T(512)(128)(4,1)S(1)} %get-tuple-element.106, ...), kind=kLoop, calls=%fused_computation.46 | loop fusion | flops 17825792 | bytes 4198656 | tf_op jit(solution)/shard_map/jit(_where)/select_n | solution.py:28
  136.3 0.2 fusion.76
  136.5 1.6 convolution_convert_fusion.1
  138.1 2.8 collective-permute-start.2
  140.9 0.0 all-gather.2.cloned.1.call-update
  141.1 106.9 %collective-permute-done.2 = bf16[4096,256]{0,1:T(8,128)(2,1)} collective-permute-done((bf16[4096,256]{0,1:T(8,128)(2,1)S(1)}, bf16[4096,256]{0,1:T(8,128)(2,1)}, u32[]{:S(2)}, u32[]{:S(2)}) %collective-permute-start.2) | collective-permute-done | bytes 2097184 | tf_op jit(solution)/shard_map/ppermute | solution.py:12
  248.1 1.9 broadcast_select_fusion.5
  249.9 16.7 %select_select_fusion.1 = bf16[4096,256]{0,1:T(8,128)(2,1)S(1)} fusion(bf16[4096,256]{0,1:T(8,128)(2,1)S(1)} %get-tuple-element.11, pred[256]{0:T(512)(128)(4,1)S(1)} %get-tuple-element.142, pred[256]{0:T(512)(128)(4,1)S(1)} %get-tuple-element.60, pred[256]{0:T(512)(128)(4,1)S(1)} %get-tuple-element.59, pred[256]{0:T(512)(128)(4,1)S(1)} %get-tuple-element.58, ...), kind=kLoop, calls=%fused_computation.41 | loop fusion | flops 17825792 | bytes 4198656 | tf_op jit(solution)/shard_map/jit(_where)/select_n | solution.py:28
  266.7 0.2 fusion.73
  266.9 16.6 %select_select_fusion = bf16[4096,256]{0,1:T(8,128)(2,1)S(1)} fusion(bf16[4096,256]{0,1:T(8,128)(2,1)S(1)} %get-tuple-element.12, pred[256]{0:T(512)(128)(4,1)S(1)} %get-tuple-element.141, pred[256]{0:T(512)(128)(4,1)S(1)} %get-tuple-element.76, pred[256]{0:T(512)(128)(4,1)S(1)} %get-tuple-element.75, pred[256]{0:T(512)(128)(4,1)S(1)} %get-tuple-element.74, ...), kind=kLoop, calls=%fused_computation.36 | loop fusion | flops 17825792 | bytes 4198656 | tf_op jit(solution)/shard_map/jit(_where)/select_n | solution.py:28
  283.5 0.2 fusion.74
  283.7 1.6 convolution_convert_fusion
  285.3 1.6 copy.13
  286.8 4.7 %all-to-all-start = ((bf16[1,4,8,128,256]{4,3,1,0,2:T(8,128)(2,1)}), bf16[1,4,8,128,256]{4,3,1,0,2:T(8,128)(2,1)S(1)}, u32[]{:S(2)}, u32[]{:S(2)}) async-start(bf16[1,4,8,128,256]{4,3,1,0,2:T(8,128)(2,1)} %copy.13), calls=%async_computation | async-start | bytes 4194304 | tf_op jit(solution)/shard_map/all_to_all | solution.py:70
  291.5 0.0 reduce-scatter.2.cloned.1.call-start
  291.5 0.0 all-gather.2.cloned.1.call-done
  291.6 0.0 copy-start
  291.6 1.4 fusion.69
  293.0 0.5 copy-done
  293.5 1.6 slice_bitcast_fusion
  295.0 45.5 %all-to-all-done = bf16[1,4,8,128,256]{4,3,1,0,2:T(8,128)(2,1)S(1)} async-done(((bf16[1,4,8,128,256]{4,3,1,0,2:T(8,128)(2,1)}), bf16[1,4,8,128,256]{4,3,1,0,2:T(8,128)(2,1)S(1)}, u32[]{:S(2)}, u32[]{:S(2)}) %all-to-all-start) | async-done | bytes 2097184 | tf_op jit(solution)/shard_map/all_to_all | solution.py:70
  340.5 5.5 %fusion.32 = f32[512,1024]{1,0:T(8,128)} fusion(bf16[8,512,256]{2,1,0:T(8,128)(2,1)S(1)} %bitcast.59, bf16[8,128,512]{2,1,0:T(8,128)(2,1)} %get-tuple-element.18, bf16[8,128,512]{2,1,0:T(8,128)(2,1)S(1)} %fusion.69, bf16[8,128,512]{2,1,0:T(8,128)(2,1)} %get-tuple-element.17), kind=kOutput, calls=%fused_computation.72 | convolution fusion | flops 2164260864 | bytes 7340032 | tf_op jit(solution)/shard_map/jrk,jkx->rx/dot_general | solution.py:74
  346.0 0.0 reduce-scatter.2.cloned.1.call-update
  346.1 34.2 %reduce-scatter.2.cloned.1.call-done = f32[128,1024]{1,0:T(8,128)} async-done(((f32[512,1024]{1,0:T(8,128)}), f32[128,1024]{1,0:T(8,128)}) %reduce-scatter.2.cloned.1.call-update) | async-done | bytes 524304 | tf_op jit(solution)/shard_map/reduce_scatter | solution.py:75
  (34 shorter events, 0.5 us)
Async XLA Ops:
  6.5 285.0 %all-gather.2.cloned.1.call-start = ((), (), s32[]{:S(2)}) async-start(), calls=%async_computation.2 | async-start | bytes 2359296 | tf_op jit(solution)/shard_map/all_gather | solution.py:72
  8.1 3.0 copy-start.3
  8.1 3.2 copy-start.1
  8.1 3.2 copy-start.2
  10.5 4.5 %collective-permute-start = (bf16[4096,256]{0,1:T(8,128)(2,1)S(1)}, bf16[4096,256]{0,1:T(8,128)(2,1)}, u32[]{:S(2)}, u32[]{:S(2)}) collective-permute-start(bf16[4096,256]{0,1:T(8,128)(2,1)S(1)} %fusion), channel_id=1, source_target_pairs={{0,1},{1,0},{2,3},{3,2},{4,5},{5,4},{6,7},{7,6},{8,9},{9,8},{10,11... | collective-permute-start | bytes 6291464 | tf_op jit(solution)/shard_map/ppermute | solution.py:12
  52.0 49.0 %collective-permute-start.1 = (bf16[4096,256]{0,1:T(8,128)(2,1)S(1)}, bf16[4096,256]{0,1:T(8,128)(2,1)}, u32[]{:S(2)}, u32[]{:S(2)}) collective-permute-start(bf16[4096,256]{0,1:T(8,128)(2,1)S(1)} %convolution_convert_fusion.2), channel_id=1, source_target_pairs={{0,2},{1,3},{2,0},{3,1},{4,6},{5,7},{6,4},{7,5},{8,10},{9,11},{10,... | collective-permute-start | bytes 6291464 | tf_op jit(solution)/shard_map/ppermute | solution.py:12
  138.1 110.0 %collective-permute-start.2 = (bf16[4096,256]{0,1:T(8,128)(2,1)S(1)}, bf16[4096,256]{0,1:T(8,128)(2,1)}, u32[]{:S(2)}, u32[]{:S(2)}) collective-permute-start(bf16[4096,256]{0,1:T(8,128)(2,1)S(1)} %convolution_convert_fusion.1), channel_id=1, source_target_pairs={{0,4},{1,5},{2,6},{3,7},{4,0},{5,1},{6,2},{7,3},{8,12},{9,13},{10,... | collective-permute-start | bytes 6291464 | tf_op jit(solution)/shard_map/ppermute | solution.py:12
  286.8 53.7 %all-to-all-start = ((bf16[1,4,8,128,256]{4,3,1,0,2:T(8,128)(2,1)}), bf16[1,4,8,128,256]{4,3,1,0,2:T(8,128)(2,1)S(1)}, u32[]{:S(2)}, u32[]{:S(2)}) async-start(bf16[1,4,8,128,256]{4,3,1,0,2:T(8,128)(2,1)} %copy.13), calls=%async_computation | async-start | bytes 4194304 | tf_op jit(solution)/shard_map/all_to_all | solution.py:70
  291.5 88.8 %reduce-scatter.2.cloned.1.call-start = ((), (), s32[]{:S(2)}) async-start(), calls=%async_computation.3 | async-start | bytes 2621440 | tf_op jit(solution)/shard_map/reduce_scatter | solution.py:75
  291.6 1.9 copy-start
Sparse Core Ops, SparseCore 0:
  141.1 72.8 all-gather.1
  346.2 34.0 reduce-scatter.1
where the time goes:
time: 388 us; the launch traced here: 387 us
  waiting for transfers between devices  236 us (61%)
  other arithmetic  108 us (28%)
  between operations  13.8 us (4%)
  matrix products  12.6 us (3%)
  starting transfers between devices  11.1 us (3%)
  local copies, waits for them, and re-layouts  5.74 us (1%)
    ppermute x3, waiting for transfers between devices, partner_2(): return lax.ppermute(value, axis, pairs)  156 us
    select_n x6, other arithmetic, shift_rows(): result = jnp.where(doubled[None, :] == offset, window, result)  99.6 us
    all_to_all x1, waiting for transfers between devices, body(): lax.all_to_all(arranged, 'tile', split_axis=2, concat_axis=0, tiled=True)  45.5 us
    reduce_scatter x1, waiting for transfers between devices, body(): lax.psum_scatter(partial_rows, 'pulse', scatter_dimension=0, tiled=True)  34.2 us
  transfers between devices with their start and end apart: 6, of which 5 were waited for; matrix products, arithmetic and copies ran while one was open for 11% of the time, Pallas kernels for 0%

commit v1 on v0

v1 whole, which is shorter than its diff:
```python
import functools

import jax
import jax.numpy as jnp
from jax import lax
from jax.experimental import pallas as pl
from jax.experimental.pallas import tpu as pltpu
from jax.sharding import PartitionSpec as P

SHIFT = 8
PAD = 16
MESH = pl.DeviceIdType.MESH
F32 = jnp.float32
BF16 = jnp.bfloat16


def bit_of(index, place):
    return index // 2**place % 2


def flip(index, place):
    return index + (1 - 2 * bit_of(index, place)) * 2**place


def complex_block(real_part, imag_part):
    upper_half = jnp.concatenate([real_part, imag_part], axis=1)
    lower_half = jnp.concatenate([-imag_part, real_part], axis=1)
    return jnp.concatenate([upper_half, lower_half], axis=0)


def orders(pulse_bits, tile_bits):
    pulse = [("pulse", place) for place in range(pulse_bits)]
    tile = [("tile", place) for place in range(1, tile_bits)]
    return [pulse + tile, pulse[::-1] + tile]


def shifted(ref, start, rows, table):
    piece = ref[pl.ds(start, rows + 2 * PAD), :].astype(F32)[PAD - SHIFT :]
    held = piece.shape[0]
    for step in (1, 2, 4):
        piece = jnp.where((table & step) != 0, pltpu.roll(piece, held - step, 0), piece)
    piece = jnp.where((table & 8) != 0, piece[8 : rows + 24], piece[: rows + 16])
    return jnp.where((table & 16) != 0, piece[16 : rows + 16], piece[:rows]).astype(BF16)


def kernel(
    pulse_bits, tile_bits, block_rows, width,
    rows_ref, steer_ref, w0_ref, w1_ref, w2_ref, map_ref, table_ref, out_ref,
    b0, bp, b1, b2, b3, map_in, own, other, final, acc, send, recv,
    beam_s, beam_r, map_s, map_r, n_s, n_r, sum_s, sum_r,
):
    p, t = lax.axis_index("pulse"), lax.axis_index("tile")
    where = {"pulse": p, "tile": t}
    total = rows_ref.shape[0]
    beams = map_ref.shape[1]
    columns = map_ref.shape[2]
    chunks = 2 * columns // width
    streams = orders(pulse_bits, tile_bits)
    steps = pulse_bits + tile_bits
    tile = 512

    def device(axis, place):
        found = dict(where)
        found[axis] = flip(where[axis], place)
        return (found["pulse"], found["tile"])

    partners = [("pulse", place) for place in range(pulse_bits)]
    partners += [("tile", place) for place in range(tile_bits)]
    barrier = pltpu.get_barrier_semaphore()
    for axis, place in partners:
        pl.semaphore_signal(barrier, inc=1, device_id=device(axis, place), device_id_type=MESH)
    for ref in (b0, bp, b1, b2):
        edge = jnp.zeros((PAD, ref.shape[1]), BF16)
        ref[0:PAD, :] = edge
        ref[PAD + total : 2 * PAD + total, :] = edge
    pl.semaphore_wait(barrier, len(partners))

    map_copy = pltpu.make_async_remote_copy(
        src_ref=map_ref, dst_ref=map_in, send_sem=map_s, recv_sem=map_r,
        device_id=device("tile", 2), device_id_type=MESH,
    )
    map_copy.start()

    parts = 4
    part = total // parts
    beam_copies = []
    for piece in range(parts):

        @pl.loop(0, part // tile)
        def _(i, piece=piece):
            start = pl.multiple_of(piece * part + i * tile, tile)
            b0[pl.ds(start + PAD, tile), :] = jnp.dot(
                rows_ref[pl.ds(start, tile), :], steer_ref[...], preferred_element_type=F32
            ).astype(BF16)

        span = pl.ds(PAD + piece * part, part)
        copy = pltpu.make_async_remote_copy(
            src_ref=b0.at[span, :], dst_ref=bp.at[span, :],
            send_sem=beam_s.at[piece], recv_sem=beam_r.at[piece],
            device_id=device("tile", 0), device_id_type=MESH,
        )
        copy.start()
        beam_copies.append(copy)
    for copy in beam_copies:
        copy.wait_recv()

    @pl.loop(0, total // tile)
    def _(i):
        start = pl.multiple_of(i * tile, tile)
        mine = shifted(b0, start, tile, table_ref[0:1, : 2 * beams])
        theirs = shifted(bp, start, tile, table_ref[1:2, : 2 * beams])
        merged = jnp.dot(mine, w0_ref[: 2 * beams, :], preferred_element_type=F32)
        merged += jnp.dot(theirs, w0_ref[2 * beams :, :], preferred_element_type=F32)
        b1[pl.ds(start + PAD, tile), :] = merged.astype(BF16)

    map_copy.wait_recv()
    weights = [w2_ref[i] for i in range(4)]

    def product(left, right):
        return jnp.dot(left, right, preferred_element_type=F32)

    own[0] = (
        product(weights[0], map_ref[0]) - product(weights[1], map_ref[1])
        + product(weights[2], map_in[0]) - product(weights[3], map_in[1])
    ).astype(BF16)
    own[1] = (
        product(weights[0], map_ref[1]) + product(weights[1], map_ref[0])
        + product(weights[2], map_in[1]) + product(weights[3], map_in[0])
    ).astype(BF16)
    n_copy = pltpu.make_async_remote_copy(
        src_ref=own, dst_ref=other, send_sem=n_s, recv_sem=n_r,
        device_id=device("tile", 1), device_id_type=MESH,
    )
    n_copy.start()

    @pl.loop(0, total // tile)
    def _(i):
        start = pl.multiple_of(i * tile, tile)
        mine = shifted(b1, start, tile, table_ref[2:3, : 2 * beams])
        b2[pl.ds(start + PAD, tile), :] = jnp.dot(
            mine, w1_ref[...], preferred_element_type=F32
        ).astype(BF16)

    @pl.loop(0, total // tile)
    def _(i):
        start = pl.multiple_of(i * tile, tile)
        b3[pl.ds(start, tile), :] = shifted(b2, start, tile, table_ref[3:4, :])

    n_copy.wait_recv()
    for at, source in ((0, own), (2 * beams, other)):
        final[at : at + beams, :columns] = source[0]
        final[at : at + beams, columns:] = source[1]
        final[at + beams : at + 2 * beams, :columns] = -source[1]
        final[at + beams : at + 2 * beams, columns:] = source[0]

    core = bit_of(t, 0)
    half = total // 2
    bases = [total - (total >> step) for step in range(steps)]
    copies = {}

    def launch(step, chunk, axis, place):
        span = pl.ds(bases[step], half >> step)
        copies[step, chunk] = copy = pltpu.make_async_remote_copy(
            src_ref=send.at[chunk, span, :], dst_ref=recv.at[chunk, span, :],
            send_sem=sum_s.at[step, chunk], recv_sem=sum_r.at[step, chunk],
            device_id=device(axis, place), device_id_type=MESH,
        )
        copy.start()

    def form(chunk_set):
        first = chunk_set[0] * width
        last = first + len(chunk_set) * width

        @pl.loop(0, total // tile)
        def _(i):
            start = pl.multiple_of(i * tile, tile)
            value = jnp.dot(
                b3[pl.ds(start, tile), :], final[:, first:last], preferred_element_type=F32
            )
            for pair in range(tile // (2 * block_rows)):
                low = value[2 * pair * block_rows : (2 * pair + 1) * block_rows]
                high = value[(2 * pair + 1) * block_rows : (2 * pair + 2) * block_rows]
                keep = jnp.where(core == 0, low, high)
                leave = jnp.where(core == 0, high, low).astype(BF16)
                number = i * (tile // (2 * block_rows)) + pair
                for at, chunk in enumerate(chunk_set):
                    order = streams[chunk % len(streams)]
                    index = 0
                    for axis, place in order:
                        where_bit = place - 1 if axis == "tile" else place + tile_bits - 1
                        index = index * 2 + bit_of(number, where_bit)
                    span = pl.ds(pl.multiple_of(index * block_rows, block_rows), block_rows)
                    acc[chunk, span, :] = keep[:, at * width : (at + 1) * width]
                    send[chunk, span, :] = leave[:, at * width : (at + 1) * width]

        for chunk in chunk_set:
            launch(0, chunk, "tile", 0)

    bases_live = {chunk: 0 for chunk in range(chunks)}

    def fold(step, chunk):
        copies[step, chunk].wait_recv()
        rows = half >> step
        live = bases_live[chunk]
        if step == steps - 1:
            span = pl.ds(pl.multiple_of(live, rows), rows)
            got = recv[chunk, pl.ds(bases[step], rows), :].astype(F32)
            out_ref[:, chunk * width : (chunk + 1) * width] = acc[chunk, span, :] + got
            return
        axis, place = streams[chunk % len(streams)][step]
        rest = rows // 2
        kept = bit_of(where[axis], place)
        size = min(rest, 256)

        @pl.loop(0, rest // size)
        def _(i):
            at = (1 - kept) * rest + i * size
            value = acc[chunk, pl.ds(pl.multiple_of(live + at, size), size), :]
            value += recv[chunk, pl.ds(pl.multiple_of(bases[step] + at, size), size), :].astype(F32)
            to = pl.ds(pl.multiple_of(bases[step + 1] + i * size, size), size)
            send[chunk, to, :] = value.astype(BF16)

        launch(step + 1, chunk, axis, place)

        @pl.loop(0, rest // size)
        def _(i):
            at = kept * rest + i * size
            span = pl.ds(pl.multiple_of(live + at, size), size)
            got = recv[chunk, pl.ds(pl.multiple_of(bases[step] + at, size), size), :]
            acc[chunk, span, :] += got.astype(F32)

        bases_live[chunk] = live + kept * rest

    sets = [[2 * i, 2 * i + 1] for i in range(chunks // 2)]
    for i, chunk_set in enumerate(sets):
        form(chunk_set)
        if i > 0:
            for chunk in sets[i - 1]:
                fold(0, chunk)
    for chunk in sets[-1]:
        fold(0, chunk)
    for step in range(1, steps):
        for chunk in range(chunks):
            fold(step, chunk)

    map_copy.wait_send()
    n_copy.wait_send()
    for copy in beam_copies:
        copy.wait_send()
    for copy in copies.values():
        copy.wait_send()


def body(pulses, steering, merge_re, merge_im, range_shift, image_map):
    total, beams = pulses.shape[0], steering.shape[2]
    pulse_size, tile_size = lax.axis_size("pulse"), lax.axis_size("tile")
    pulse_bits, tile_bits = pulse_size.bit_length() - 1, tile_size.bit_length() - 1
    block_rows = total // (pulse_size * tile_size)
    columns = image_map.shape[4]
    width = 128
    chunks = 2 * columns // width
    steps = pulse_bits + tile_bits
    t = lax.axis_index("tile")
    bits = [t >> level & 1 for level in range(3)]

    def weight(level, source, target):
        take = lambda array: lax.dynamic_slice(
            array[level], (source * beams, target * beams), (beams, beams)
        )
        return take(merge_re), take(merge_im)

    steer = complex_block(steering[0], steering[1])
    w0 = jnp.concatenate(
        [complex_block(*weight(0, s, bits[0])) for s in (bits[0], 1 - bits[0])], axis=0
    )
    w1 = jnp.concatenate(
        [complex_block(*weight(1, bits[1], h)) for h in (bits[1], 1 - bits[1])], axis=1
    )
    w2 = jnp.stack([*weight(2, bits[2], bits[2]), *weight(2, bits[2], 1 - bits[2])])
    take = lambda level, source: lax.dynamic_index_in_dim(
        range_shift[level], source, 0, keepdims=False
    )
    table = jnp.stack(
        [
            jnp.tile(take(level, source), 4)
            for level, source in ((0, bits[0]), (0, 1 - bits[0]), (1, bits[1]), (2, bits[2]))
        ]
    ) + SHIFT
    vmem = pl.BlockSpec(memory_space=pltpu.VMEM)
    dma = pltpu.SemaphoreType.DMA
    padded = total + 2 * PAD
    return pl.pallas_call(
        functools.partial(kernel, pulse_bits, tile_bits, block_rows, width),
        out_shape=jax.ShapeDtypeStruct((block_rows, 2 * columns), F32),
        in_specs=[vmem] * 7,
        out_specs=vmem,
        scratch_shapes=[
            pltpu.VMEM((padded, 2 * beams), BF16),
            pltpu.VMEM((padded, 2 * beams), BF16),
            pltpu.VMEM((padded, 2 * beams), BF16),
            pltpu.VMEM((padded, 4 * beams), BF16),
            pltpu.VMEM((total, 4 * beams), BF16),
            pltpu.VMEM((2, beams, columns), BF16),
            pltpu.VMEM((2, beams, columns), BF16),
            pltpu.VMEM((2, beams, columns), BF16),
            pltpu.VMEM((4 * beams, 2 * columns), BF16),
            pltpu.VMEM((chunks, total // 2, width), F32),
            pltpu.VMEM((chunks, total, width), BF16),
            pltpu.VMEM((chunks, total, width), BF16),
            dma((4,)),
            dma((4,)),
            dma,
            dma,
            dma,
            dma,
            dma((steps, chunks)),
            dma((steps, chunks)),
        ],
        compiler_params=pltpu.CompilerParams(
            collective_id=0, has_side_effects=True, vmem_limit_bytes=60 * 2**20
        ),
    )(pulses.reshape(total, -1), steer, w0, w1, w2, image_map[0, 0], table)


def solution(mesh):
    placed = (
        P(None, None, ("pulse", "tile")),
        P(),
        P(),
        P(),
        P(),
        P("pulse", "tile", None, None, None),
    )
    return jax.shard_map(
        body, mesh=mesh, in_specs=placed, out_specs=P(("pulse", "tile"), None), check_vma=False
    )
```

time: 388 us -> 95.4 us (0.25)
  waiting for transfers between devices: 236 us -> 0 us
  other arithmetic: 108 us -> 4.22 us
  Pallas kernels: 0 us -> 83.6 us
  between operations: 13.8 us -> 0.08 us
  matrix products: 12.6 us -> 0 us
  starting transfers between devices: 11.1 us -> 0 us
    ppermute x3 -> x0, waiting for transfers between devices: 156 us -> none  [partner_2(): return lax.ppermute(value, axis, pairs)]
    select_n x9 -> x0, other arithmetic: 105 us -> none  [the longest x6 99.6 us: shift_rows(): result = jnp.where(doubled[None, :] == offset, window, result)]
    pallas_call x0 -> x1, Pallas kernels: none -> 83.6 us  [body(): pl.pallas_call(functools.partial(kernel, pulse_bits, tile_bits, block_row...]
    all_to_all x1 -> x0, waiting for transfers between devices: 45.5 us -> none  [body(): lax.all_to_all(arranged, 'tile', split_axis=2, concat_axis=0, tiled=True)]
    reduce_scatter x1 -> x0, waiting for transfers between devices: 34.2 us -> none  [body(): lax.psum_scatter(partial_rows, 'pulse', scatter_dimension=0, tiled=True)]
    dot_general x5 -> x0, matrix products: 12.6 us -> none  [the longest x1 5.52 us: body(): jnp.einsum('jrk,jkx->rx', received, blocks, preferred_element_type=jnp.fl...]
    ppermute x3 -> x0, starting transfers between devices: 6.37 us -> none  [partner_2(): return lax.ppermute(value, axis, pairs)]
    all_to_all x1 -> x0, starting transfers between devices: 4.66 us -> none  [body(): lax.all_to_all(arranged, 'tile', split_axis=2, concat_axis=0, tiled=True)]
  transfers between devices with their start and end apart: 6 -> 0, of which waited for: 5 -> 0; matrix products, arithmetic and copies ran while one was open for 11% -> 0% of each run, Pallas kernels for 0% -> 0%
where the time goes in v1:
time: 95.4 us; the launch traced here: 95.1 us
  Pallas kernels  83.6 us (88%)
  local copies, waits for them, and re-layouts  7.22 us (8%)
  other arithmetic  4.22 us (4%)
    pallas_call x1, Pallas kernels, body(): pl.pallas_call(functools.partial(kernel, pulse_bits, tile_bits, block_row...  83.6 us
    unnamed x4, local copies, waits for them, and re-layouts  3.51 us
    slice x2, local copies, waits for them, and re-layouts, weight(): array[level]  2.12 us

profile of v1, /device:TPU:0, one launch (start us, length us, event | category | flops | bytes accessed | tf_op | source)
XLA Modules:
  0.0 95.1 jit_solution(2065978736636386553)
XLA Ops:
  0.0 0.7 fusion.11
  0.7 0.0 copy-start
  0.8 0.6 add_add_fusion.table_ref
  1.4 0.8 fusion.4
  2.2 0.8 slice_bitcast_fusion
  2.9 0.7 maximum_maximum_fusion.2.steer_ref
  3.6 1.1 %fusion.9 = (bf16[1,256,256]{2,1,0:T(8,128)(2,1)S(1)}, bf16[1,256,256]{2,1,0:T(8,128)(2,1)S(1)}, bf16[1,256,256]{2,1,0:T(8,128)(2,1)S(1)}) fusion(bf16[3,256,256]{2,1,0:T(8,128)(2,1)} %param.8), kind=kLoop, calls=%fused_computation.33 | loop fusion | bytes 786432 | tf_op jit(solution)/shard_map/slice | solution.py:268
  4.7 1.1 %fusion.10 = (bf16[1,256,256]{2,1,0:T(8,128)(2,1)S(1)}, bf16[1,256,256]{2,1,0:T(8,128)(2,1)S(1)}, bf16[1,256,256]{2,1,0:T(8,128)(2,1)S(1)}) fusion(bf16[3,256,256]{2,1,0:T(8,128)(2,1)} %param.9), kind=kLoop, calls=%fused_computation.34 | loop fusion | bytes 786432 | tf_op jit(solution)/shard_map/slice | solution.py:268
  5.8 0.7 pad_maximum_fusion.w2_ref
  6.5 0.7 maximum_maximum_fusion.1.w1_ref
  7.3 0.7 maximum_maximum_fusion.w0_ref
  8.0 0.0 copy-done
  8.0 1.6 %copy.9 = bf16[512,8,2,128]{3,1,2,0:T(8,128)(2,1)} copy(bf16[512,8,2,128]{3,2,1,0:T(2,128)(2,1)S(1)} %bitcast.44) | data formatting | bytes 4194304
  9.6 83.6 %shard_map.64 = f32[128,1024]{1,0:T(8,128)} custom-call(bf16[4096,256]{1,0:T(8,128)(2,1)} %bitcast.43, bf16[256,256]{1,0:T(8,128)(2,1)} %maximum_maximum_fusion.2.steer_ref, bf16[512,256]{1,0:T(8,128)(2,1)} %maximum_maximum_fusion.w0_ref, bf16[256,512]{1,0:T(8,128)(2,1)} %maximum_maximum_fusion.1.w1_ref, bf16[4,128,128]{2,1,0:T(8,128)(2,1)} %pad_maximum_fusion.w2_ref, ...), custom_call_target="tpu_custom_call" | custom-call | tf_op jit(solution)/shard_map/pallas_call | solution.py:292
  93.2 1.9 %copy.11 = f32[128,1024]{1,0:T(8,128)} copy(f32[128,1024]{1,0:T(8,128)} %shard_map.64) | data formatting | bytes 1048576
  (9 shorter events, 0.1 us)
Async XLA Ops:
  0.7 7.3 %copy-start = (bf16[4096,2,128]{2,1,0:T(2,128)(2,1)S(1)}, bf16[4096,2,128]{2,1,0:T(2,128)(2,1)}, u32[]{:S(2)}) copy-start(bf16[4096,2,128]{2,1,0:T(2,128)(2,1)} %param.6) | copy-start | bytes 6291460

commit v2 on v1

v2 whole, which is shorter than its diff:
```python
import functools

import jax
import jax.numpy as jnp
from jax import lax
from jax.experimental import pallas as pl
from jax.experimental.pallas import tpu as pltpu
from jax.sharding import PartitionSpec as P

SHIFT = 8
PAD = 16
STRIP = 128
MESH = pl.DeviceIdType.MESH
F32 = jnp.float32
BF16 = jnp.bfloat16


def bit_of(index, place):
    return index // 2**place % 2


def flip(index, place):
    return index + (1 - 2 * bit_of(index, place)) * 2**place


def orders(pulse_bits, tile_bits):
    pulse = [("pulse", place) for place in range(pulse_bits)]
    tile = [("tile", place) for place in range(1, tile_bits)]
    return [
        pulse + tile, pulse[::-1] + tile, tile + pulse,
        pulse + tile, pulse[::-1] + tile, tile + pulse[::-1],
        pulse + tile, pulse[::-1] + tile,
    ]


def shifted(ref, start, rows, table):
    columns = []
    for column in range(0, ref.shape[1], 128):
        shift = table[:, column : column + 128]
        masks = [(shift & step) != 0 for step in (1, 2, 4, 8, 16)]
        strips = []
        for strip in range(0, rows, STRIP):
            piece = ref[pl.ds(start + strip, STRIP + 2 * PAD), column : column + 128]
            piece = piece.astype(F32)[PAD - SHIFT :]
            held = piece.shape[0]
            for mask, step in zip(masks, (1, 2, 4)):
                piece = jnp.where(mask, pltpu.roll(piece, held - step, 0), piece)
            piece = jnp.where(masks[3], piece[8 : STRIP + 24], piece[: STRIP + 16])
            piece = jnp.where(masks[4], piece[16 : STRIP + 16], piece[:STRIP])
            strips.append(piece.astype(BF16))
        columns.append(jnp.concatenate(strips, axis=0))
    return jnp.concatenate(columns, axis=1)


def kernel(
    pulse_bits, tile_bits, block_rows, width,
    rows_ref, steer_ref, re_ref, im_ref, shift_ref, map_ref, out_ref,
    real, imag, w0_ref, w1_ref, w2_ref, b0, bp, b1, b2, b3, map_in, own, other, final, acc, send, recv,
    beam_s, beam_r, map_s, map_r, n_s, n_r, sum_s, sum_r,
):
    p, t = lax.axis_index("pulse"), lax.axis_index("tile")
    where = {"pulse": p, "tile": t}
    total = rows_ref.shape[0] // 2
    beams = map_ref.shape[1]
    columns = map_ref.shape[2]
    pieces = columns // width
    chunks = 2 * pieces
    streams = orders(pulse_bits, tile_bits)
    steps = pulse_bits + tile_bits
    tile = 512
    bits = [bit_of(t, level) for level in range(3)]

    def device(axis, place):
        found = dict(where)
        found[axis] = flip(where[axis], place)
        return (found["pulse"], found["tile"])

    partners = [("pulse", place) for place in range(pulse_bits)]
    partners += [("tile", place) for place in range(tile_bits)]
    barrier = pltpu.get_barrier_semaphore()
    for axis, place in partners:
        pl.semaphore_signal(barrier, inc=1, device_id=device(axis, place), device_id_type=MESH)

    def product(left, right):
        return jnp.dot(left, right, preferred_element_type=F32)

    part = total // 4

    def steer(piece):
        @pl.loop(0, part // tile)
        def _(i):
            start = pl.multiple_of(piece * part + i * tile, tile)
            both = rows_ref[pl.ds(2 * start, 2 * tile), :]
            real[...] = product(both, steer_ref[0])
            imag[...] = product(both, steer_ref[1])
            even, odd = pl.ds(0, tile, stride=2), pl.ds(1, tile, stride=2)
            to = pl.ds(start + PAD, tile)
            b0[to, :beams] = (real[even, :] - imag[odd, :]).astype(BF16)
            b0[to, beams:] = (imag[even, :] + real[odd, :]).astype(BF16)

    for ref in (b0, bp, b1, b2):
        edge = jnp.zeros((PAD, ref.shape[1]), BF16)
        ref[0:PAD, :] = edge
        ref[PAD + total : 2 * PAD + total, :] = edge
    steer(0)
    pl.semaphore_wait(barrier, len(partners))

    def span_of(piece):
        return slice(piece * width, (piece + 1) * width)

    map_copies = [
        pltpu.make_async_remote_copy(
            src_ref=map_ref.at[:, :, span_of(piece)], dst_ref=map_in.at[:, :, span_of(piece)],
            send_sem=map_s.at[piece], recv_sem=map_r.at[piece],
            device_id=device("tile", 2), device_id_type=MESH,
        )
        for piece in range(pieces)
    ]
    n_copies = [
        pltpu.make_async_remote_copy(
            src_ref=own.at[:, :, span_of(piece)], dst_ref=other.at[:, :, span_of(piece)],
            send_sem=n_s.at[piece], recv_sem=n_r.at[piece],
            device_id=device("tile", 1), device_id_type=MESH,
        )
        for piece in range(pieces)
    ]
    beam_copies = [
        pltpu.make_async_remote_copy(
            src_ref=b0.at[pl.ds(PAD + piece * part, part), :],
            dst_ref=bp.at[pl.ds(PAD + piece * part, part), :],
            send_sem=beam_s.at[piece], recv_sem=beam_r.at[piece],
            device_id=device("tile", 0), device_id_type=MESH,
        )
        for piece in range(4)
    ]
    for copy in map_copies:
        copy.start()
    beam_copies[0].start()
    for piece in range(1, 4):
        steer(piece)
        beam_copies[piece].start()

    def weight(level, source, target):
        at = (level, pl.ds(pl.multiple_of(source * beams, beams), beams))
        at += (pl.ds(pl.multiple_of(target * beams, beams), beams),)
        return re_ref[at], im_ref[at]

    def put_block(ref, row, column, parts):
        ref[row : row + beams, column : column + beams] = parts[0]
        ref[row : row + beams, column + beams : column + 2 * beams] = parts[1]
        ref[row + beams : row + 2 * beams, column : column + beams] = -parts[1]
        ref[row + beams : row + 2 * beams, column + beams : column + 2 * beams] = parts[0]

    def offsets(level, source):
        line = jnp.where(source == 0, shift_ref[level, 0:1, :], shift_ref[level, 1:2, :])
        return jnp.concatenate([line, line], axis=1) + SHIFT

    for at, flipped in ((0, bits[0]), (2 * beams, 1 - bits[0])):
        put_block(w0_ref, at, 0, weight(0, flipped, bits[0]))
    for at, flipped in ((0, bits[1]), (2 * beams, 1 - bits[1])):
        put_block(w1_ref, 0, at, weight(1, bits[1], flipped))
    for at, flipped in ((0, bits[2]), (2, 1 - bits[2])):
        w2_ref[at], w2_ref[at + 1] = weight(2, bits[2], flipped)

    tables = [offsets(0, bits[0]), offsets(0, 1 - bits[0]), offsets(1, bits[1]), offsets(2, bits[2])]

    def level_0(low, high):
        @pl.loop(low, high)
        def _(i):
            start = pl.multiple_of(i * tile, tile)
            mine = shifted(b0, start, tile, tables[0])
            theirs = shifted(bp, start, tile, tables[1])
            merged = product(mine, w0_ref[: 2 * beams, :])
            merged += product(theirs, w0_ref[2 * beams :, :])
            b1[pl.ds(start + PAD, tile), :] = merged.astype(BF16)

    done = 0
    for piece in range(4):
        beam_copies[piece].wait_recv()
        reach = total // tile if piece == 3 else (piece + 1) * part // tile - 1
        level_0(done, reach)
        done = reach

    def compose(piece):
        span = span_of(piece)
        map_copies[piece].wait_recv()
        left = [w2_ref[i] for i in range(4)]
        right = [map_ref[0, :, span], map_ref[1, :, span], map_in[0, :, span], map_in[1, :, span]]
        own[0, :, span] = (
            product(left[0], right[0]) - product(left[1], right[1])
            + product(left[2], right[2]) - product(left[3], right[3])
        ).astype(BF16)
        own[1, :, span] = (
            product(left[0], right[1]) + product(left[1], right[0])
            + product(left[2], right[3]) + product(left[3], right[2])
        ).astype(BF16)
        n_copies[piece].start()

    for piece in range(pieces // 2):
        compose(piece)

    @pl.loop(0, total // tile)
    def _(i):
        start = pl.multiple_of(i * tile, tile)
        mine = shifted(b1, start, tile, tables[2])
        b2[pl.ds(start + PAD, tile), :] = product(mine, w1_ref[...]).astype(BF16)

    for piece in range(pieces // 2, pieces):
        compose(piece)

    twice = jnp.concatenate([tables[3], tables[3]], axis=1)

    @pl.loop(0, total // tile)
    def _(i):
        start = pl.multiple_of(i * tile, tile)
        b3[pl.ds(start, tile), :] = shifted(b2, start, tile, twice)

    core = bit_of(t, 0)
    half = total // 2
    bases = [total - (total >> step) for step in range(steps)]
    copies = {}

    def launch(step, chunk, axis, place):
        span = pl.ds(bases[step], half >> step)
        copies[step, chunk] = copy = pltpu.make_async_remote_copy(
            src_ref=send.at[chunk, span, :], dst_ref=recv.at[chunk, span, :],
            send_sem=sum_s.at[step, chunk], recv_sem=sum_r.at[step, chunk],
            device_id=device(axis, place), device_id_type=MESH,
        )
        copy.start()

    def form(piece):
        span = span_of(piece)
        n_copies[piece].wait_recv()
        for at, source in ((0, own), (2 * beams, other)):
            put_block(final, at, 0, (source[0, :, span], source[1, :, span]))
        chunk_set = (2 * piece, 2 * piece + 1)

        @pl.loop(0, total // tile)
        def _(i):
            start = pl.multiple_of(i * tile, tile)
            value = product(b3[pl.ds(start, tile), :], final[...])
            for pair in range(tile // (2 * block_rows)):
                low = value[2 * pair * block_rows : (2 * pair + 1) * block_rows]
                high = value[(2 * pair + 1) * block_rows : (2 * pair + 2) * block_rows]
                keep = jnp.where(core == 0, low, high)
                leave = jnp.where(core == 0, high, low).astype(BF16)
                number = i * (tile // (2 * block_rows)) + pair
                for at, chunk in enumerate(chunk_set):
                    order = streams[chunk % len(streams)]
                    index = 0
                    for axis, place in order:
                        where_bit = place - 1 if axis == "tile" else place + tile_bits - 1
                        index = index * 2 + bit_of(number, where_bit)
                    span = pl.ds(pl.multiple_of(index * block_rows, block_rows), block_rows)
                    acc[chunk, span, :] = keep[:, at * width : (at + 1) * width]
                    send[chunk, span, :] = leave[:, at * width : (at + 1) * width]

        for chunk in chunk_set:
            launch(0, chunk, "tile", 0)

    bases_live = {chunk: 0 for chunk in range(chunks)}

    def fold(step, chunk):
        copies[step, chunk].wait_recv()
        rows = half >> step
        live = bases_live[chunk]
        if step == steps - 1:
            span = pl.ds(pl.multiple_of(live, rows), rows)
            got = recv[chunk, pl.ds(bases[step], rows), :].astype(F32)
            first = chunk % 2 * columns + chunk // 2 * width
            out_ref[:, first : first + width] = acc[chunk, span, :] + got
            return
        axis, place = streams[chunk % len(streams)][step]
        rest = rows // 2
        kept = bit_of(where[axis], place)
        size = min(rest, 256)

        @pl.loop(0, rest // size)
        def _(i):
            at = (1 - kept) * rest + i * size
            value = acc[chunk, pl.ds(pl.multiple_of(live + at, size), size), :]
            value += recv[chunk, pl.ds(pl.multiple_of(bases[step] + at, size), size), :].astype(F32)
            to = pl.ds(pl.multiple_of(bases[step + 1] + i * size, size), size)
            send[chunk, to, :] = value.astype(BF16)

        launch(step + 1, chunk, axis, place)

        @pl.loop(0, rest // size)
        def _(i):
            at = kept * rest + i * size
            span = pl.ds(pl.multiple_of(live + at, size), size)
            got = recv[chunk, pl.ds(pl.multiple_of(bases[step] + at, size), size), :]
            acc[chunk, span, :] += got.astype(F32)

        bases_live[chunk] = live + kept * rest

    for piece in range(pieces):
        form(piece)
        if piece > 0:
            fold(0, 2 * piece - 2)
            fold(0, 2 * piece - 1)
    fold(0, chunks - 2)
    fold(0, chunks - 1)
    for step in range(1, steps):
        for chunk in range(chunks):
            fold(step, chunk)

    for copy in (*map_copies, *n_copies, *beam_copies, *copies.values()):
        copy.wait_send()


def body(pulses, steering, merge_re, merge_im, range_shift, image_map):
    total, beams = pulses.shape[0], steering.shape[2]
    pulse_size, tile_size = lax.axis_size("pulse"), lax.axis_size("tile")
    pulse_bits, tile_bits = pulse_size.bit_length() - 1, tile_size.bit_length() - 1
    block_rows = total // (pulse_size * tile_size)
    columns = image_map.shape[4]
    width = 128
    chunks = 2 * columns // width
    steps = pulse_bits + tile_bits
    vmem = pl.BlockSpec(memory_space=pltpu.VMEM)
    dma = pltpu.SemaphoreType.DMA
    padded = total + 2 * PAD
    return pl.pallas_call(
        functools.partial(kernel, pulse_bits, tile_bits, block_rows, width),
        out_shape=jax.ShapeDtypeStruct((block_rows, 2 * columns), F32),
        in_specs=[vmem] * 6,
        out_specs=vmem,
        scratch_shapes=[
            pltpu.VMEM((1024, beams), F32),
            pltpu.VMEM((1024, beams), F32),
            pltpu.VMEM((4 * beams, 2 * beams), BF16),
            pltpu.VMEM((2 * beams, 4 * beams), BF16),
            pltpu.VMEM((4, beams, beams), BF16),
            pltpu.VMEM((padded, 2 * beams), BF16),
            pltpu.VMEM((padded, 2 * beams), BF16),
            pltpu.VMEM((padded, 2 * beams), BF16),
            pltpu.VMEM((padded, 4 * beams), BF16),
            pltpu.VMEM((total, 4 * beams), BF16),
            pltpu.VMEM((2, beams, columns), BF16),
            pltpu.VMEM((2, beams, columns), BF16),
            pltpu.VMEM((2, beams, columns), BF16),
            pltpu.VMEM((4 * beams, 2 * width), BF16),
            pltpu.VMEM((chunks, total // 2, width), F32),
            pltpu.VMEM((chunks, total, width), BF16),
            pltpu.VMEM((chunks, total, width), BF16),
            dma((4,)),
            dma((4,)),
            dma((chunks // 2,)),
            dma((chunks // 2,)),
            dma((chunks // 2,)),
            dma((chunks // 2,)),
            dma((steps, chunks)),
            dma((steps, chunks)),
        ],
        compiler_params=pltpu.CompilerParams(
            collective_id=0, has_side_effects=True, vmem_limit_bytes=60 * 2**20
        ),
    )(pulses.reshape(2 * total, -1), steering, merge_re, merge_im, range_shift, image_map[0, 0])


def solution(mesh):
    placed = (
        P(None, None, ("pulse", "tile")),
        P(),
        P(),
        P(),
        P(),
        P("pulse", "tile", None, None, None),
    )
    return jax.shard_map(
        body, mesh=mesh, in_specs=placed, out_specs=P(("pulse", "tile"), None), check_vma=False
    )
```

time: 95.4 us -> 72.1 us (0.76)
  Pallas kernels: 83.6 us -> 70.1 us
  local copies, waits for them, and re-layouts: 7.22 us -> 1.89 us
  other arithmetic: 4.22 us -> 0 us
    pallas_call x1, Pallas kernels: 83.6 us -> 70.1 us  [body(): pl.pallas_call(functools.partial(kernel, pulse_bits, tile_bits, block_row...]
    slice x3 -> x0, local copies, waits for them, and re-layouts: 2.83 us -> none  [the longest x2 2.12 us: weight(): array[level]]
    concatenate x3 -> x0, other arithmetic: 2.14 us -> none  [the longest x1 0.73 us: body(): jnp.concatenate([complex_block(*weight(1, bits[1], h)) for h in (bits[1],...]
    unnamed x4 -> x1, local copies, waits for them, and re-layouts: 3.51 us -> 1.89 us
where the time goes in v2:
time: 72.1 us; the launch traced here: 72 us
  Pallas kernels  70.1 us (97%)
  local copies, waits for them, and re-layouts  1.89 us (3%)
    pallas_call x1, Pallas kernels, body(): pl.pallas_call(functools.partial(kernel, pulse_bits, tile_bits, block_row...  70.1 us
    unnamed x1, local copies, waits for them, and re-layouts  1.89 us

profile of v2, /device:TPU:0, one launch (start us, length us, event | category | flops | bytes accessed | tf_op | source)
XLA Modules:
  0.0 72.0 jit_solution(13703851704485725381)
XLA Ops:
  0.0 70.1 %shard_map.64 = f32[128,1024]{1,0:T(8,128)} custom-call(bf16[8192,128]{1,0:T(8,128)(2,1)} %bitcast.2, bf16[2,128,128]{2,1,0:T(8,128)(2,1)} %steer_ref.1, bf16[3,256,256]{2,1,0:T(8,128)(2,1)} %re_ref.1, bf16[3,256,256]{2,1,0:T(8,128)(2,1)} %im_ref.1, s32[3,2,128]{2,1,0:T(2,128)} %shift_ref.1, bf16[2,128,512]{2,1,0:T(8,128)(2,1)} %bitcast.3), custom_call_target="tpu_custom_call" | custom-call | tf_op jit(solution)/shard_map/pallas_call | solution.py:325
  70.1 1.9 %copy.8 = f32[128,1024]{1,0:T(8,128)} copy(f32[128,1024]{1,0:T(8,128)} %shard_map.64) | data formatting | bytes 1048576

commit v3 on v2

--- a/solution.py
+++ b/solution.py
@@ -35,19 +35,26 @@
 
 def shifted(ref, start, rows, table):
     columns = []
+    lane_rows = lax.broadcasted_iota(jnp.int32, (8, 128), 0)
     for column in range(0, ref.shape[1], 128):
-        shift = table[:, column : column + 128]
-        masks = [(shift & step) != 0 for step in (1, 2, 4, 8, 16)]
+        shift = jnp.broadcast_to(table[:, column : column + 128], (8, 128))
+        moved = lane_rows + (shift & 7)
+        index, wraps = moved & 7, moved >= 8
+        first, second = shift < 8, shift < 16
         strips = []
         for strip in range(0, rows, STRIP):
             piece = ref[pl.ds(start + strip, STRIP + 2 * PAD), column : column + 128]
-            piece = piece.astype(F32)[PAD - SHIFT :]
-            held = piece.shape[0]
-            for mask, step in zip(masks, (1, 2, 4)):
-                piece = jnp.where(mask, pltpu.roll(piece, held - step, 0), piece)
-            piece = jnp.where(masks[3], piece[8 : STRIP + 24], piece[: STRIP + 16])
-            piece = jnp.where(masks[4], piece[16 : STRIP + 16], piece[:STRIP])
-            strips.append(piece.astype(BF16))
+            piece = piece.astype(F32)
+            turned = [
+                jnp.take_along_axis(piece[at : at + 8], index, axis=0, mode="promise_in_bounds")
+                for at in range(PAD - SHIFT, STRIP + 2 * PAD, 8)
+            ]
+            joined = [jnp.where(wraps, b, a) for a, b in zip(turned, turned[1:])]
+            picked = [
+                jnp.where(first, a, jnp.where(second, b, c))
+                for a, b, c in zip(joined, joined[1:], joined[2:])
+            ]
+            strips.append(jnp.concatenate(picked, axis=0).astype(BF16))
         columns.append(jnp.concatenate(strips, axis=0))
     return jnp.concatenate(columns, axis=1)
 

time: 72.1 us -> 68.4 us (0.949)
  Pallas kernels: 70.1 us -> 66.4 us
    pallas_call x1, Pallas kernels: 70.1 us -> 66.4 us  [body(): pl.pallas_call(functools.partial(kernel, pulse_bits, tile_bits, block_row...]
where the time goes in v3:
time: 68.4 us; the launch traced here: 68.3 us
  Pallas kernels  66.4 us (97%)
  local copies, waits for them, and re-layouts  1.89 us (3%)
    pallas_call x1, Pallas kernels, body(): pl.pallas_call(functools.partial(kernel, pulse_bits, tile_bits, block_row...  66.4 us
    unnamed x1, local copies, waits for them, and re-layouts  1.89 us

profile of v3, /device:TPU:0, one launch (start us, length us, event | category | flops | bytes accessed | tf_op | source)
XLA Modules:
  0.0 68.3 jit_solution(4151457404578200771)
XLA Ops:
  0.0 66.4 %shard_map.64 = f32[128,1024]{1,0:T(8,128)} custom-call(bf16[8192,128]{1,0:T(8,128)(2,1)} %bitcast.2, bf16[2,128,128]{2,1,0:T(8,128)(2,1)} %steer_ref.1, bf16[3,256,256]{2,1,0:T(8,128)(2,1)} %re_ref.1, bf16[3,256,256]{2,1,0:T(8,128)(2,1)} %im_ref.1, s32[3,2,128]{2,1,0:T(2,128)} %shift_ref.1, bf16[2,128,512]{2,1,0:T(8,128)(2,1)} %bitcast.3), custom_call_target="tpu_custom_call" | custom-call | tf_op jit(solution)/shard_map/pallas_call | solution.py:332
  66.4 1.9 %copy.8 = f32[128,1024]{1,0:T(8,128)} copy(f32[128,1024]{1,0:T(8,128)} %shard_map.64) | data formatting | bytes 1048576
